TPU v7x, 128 devices: a whole 4x4x4 slice. The times are simulated.
128 devices in a mesh: tm: 128 (over x, z, y, core).
Axes of the slice: x: 4, y: 4, z: 4, core: 2. Of those that a mesh axis runs over, the one named last changes fastest.
Arguments:
- field: bfloat16 [43008, 8192], P('tm'), may hold values from -52 to 52
- index: float32 [43008, 10], P('tm'), may hold values from -13 to 13
- lag_list: int32 [61], replicated, may hold values from -30 to 30, as said below
- index_offset: int32 [10], replicated, may hold values from 0 to 14, as said below
- sea_mask: int32 [8192], P('tm'), may hold values 0 or 1
Outputs:
- corr_maps: float32 [8192, 10, 61], P('tm')
Inputs may be any that keep to these rules, and one draw needn't show every extreme that they name: `lag_list`: each whole number of -30 to 30 appears once. `index_offset`: some index has the extra lead 14.
All inputs are finite; a program needn't handle non-finite values. No bound on the sum of `sea_mask` on one device may be relied on, other than what follows from the above.
Results may differ from a plain program's by a relative error of at most 0.00051.
Values may be sent and summed in bfloat16 or wider, within the bound.
No kernel may reach another device: no remote copies, remote signals or barrier semaphores. Data moves between devices by JAX's collectives and lax.ppermute only.
A program may use at most 256 MiB of HBM per device.

v0:
```python
import jax
import jax.numpy as jnp
from jax import lax
from jax.sharding import Mesh
from jax.sharding import PartitionSpec as P

MAXLAG = 30
MAXOFF = 14
TM = ("tm_0", "tm_1", "tm_2", "tm_3")


def one_axis_at_a_time(array, axes):
    for axis in axes:
        array = lax.psum(array, axis)
    return array


def padded_2(array, sides, width):
    for axis, dim in sides:
        devices, length = (lax.axis_size(axis), array.shape[dim])
        up = [(i, (i + 1) % devices) for i in range(devices - 1)]
        down = [(j, i) for i, j in up]
        last = lax.slice_in_dim(array, length - width, length, axis=dim)
        initial = lax.slice_in_dim(array, 0, width, axis=dim)
        before = lax.ppermute(last, axis, up)
        after = lax.ppermute(initial, axis, down)
        array = jnp.concatenate([before, array, after], axis=dim)
    return array


def build_window_sums(padded, length, reach, lag_low):
    count = reach + lag_low + 1
    piece = lax.slice_in_dim(padded, 0, length + reach + lag_low, axis=0)
    windows = jnp.stack(
        [piece[reach + lag_low - j : reach + lag_low - j + length] for j in range(count)], 1
    )
    return windows.reshape(length, count * padded.shape[1])


def lag_selector(shifts, reach, lag_low):
    count = reach + lag_low + 1
    places = jnp.arange(count, dtype=jnp.int32)
    return (places[None, :, None] == (shifts + lag_low)[:, None, :]).astype(jnp.float32)


def pick_lags(accum, selector):
    kcount, count, lcount = selector.shape
    spread = accum.reshape(accum.shape[0], count, kcount)
    chosen = jnp.einsum("cjk,kjl->ckl", spread, selector, precision=lax.Precision.HIGHEST)
    return chosen.reshape(accum.shape[0], kcount * lcount)


def finish(products, first_sum, second_sum, prefix_totals, var_i, sea_mask, total_days):
    kcount, lcount = prefix_totals.shape
    mean_x = first_sum / total_days
    var_x = second_sum / total_days - mean_x * mean_x
    numer = products.reshape(-1, kcount, lcount) - mean_x[:, None, None] * prefix_totals[None]
    scale = (
        total_days * jnp.sqrt(var_x + 1e-06)[:, None, None] * jnp.sqrt(var_i + 1e-06)[None, :, None]
    )
    return numer / scale * sea_mask.astype(jnp.float32)[:, None, None]


def shards(field, index, lag_list, index_offset, sea_mask):
    t_dev = field.shape[0]
    devices = lax.axis_size(TM)
    day_count = t_dev * devices
    total_days = day_count * 1.0
    kcount = index.shape[1]
    reach = MAXLAG + MAXOFF
    shifts = lag_list[None, :] + index_offset[:, None]
    selector = lag_selector(shifts, reach, MAXLAG)
    first_i, second_i = (
        one_axis_at_a_time(jnp.sum(index, 0), TM),
        one_axis_at_a_time(jnp.sum(index * index, 0), TM),
    )
    mean_i = first_i / total_days
    var_i = second_i / total_days - mean_i * mean_i
    centered = (index - mean_i).astype(jnp.bfloat16)
    padded = padded_2(centered, ((TM, 0),), reach)
    windows = build_window_sums(padded, t_dev, reach, MAXLAG)
    window_sums = jnp.sum(windows.astype(jnp.float32), 0)
    local_totals = pick_lags(window_sums[None, :], selector)[0]
    prefix_totals = one_axis_at_a_time(local_totals, TM).reshape(kcount, -1)
    spread = lax.dot_general(
        field, windows, (((0,), (0,)), ((), ())), preferred_element_type=jnp.float32
    )
    wide = field.astype(jnp.float32)
    combined = lax.psum_scatter(
        jnp.concatenate(
            [
                pick_lags(spread, selector),
                jnp.sum(wide, 0)[:, None],
                jnp.sum(wide * wide, 0)[:, None],
            ],
            1,
        ),
        TM,
        scatter_dimension=0,
        tiled=True,
    )
    width_all = combined.shape[1] - 2
    products = combined[:, :width_all]
    return finish(
        products,
        combined[:, width_all],
        combined[:, width_all + 1],
        prefix_totals,
        var_i,
        sea_mask,
        total_days,
    )


def solution(mesh):
    finer = Mesh(mesh.devices.reshape(4, 4, 4, 2), ("tm_0", "tm_1", "tm_2", "tm_3"))
    return jax.shard_map(
        shards,
        mesh=finer,
        in_specs=(P(TM, None), P(TM, None), P(), P(), P(TM)),
        out_specs=P(TM, None, None),
        check_vma=False,
    )
```

profile of v0, /device:TPU:1, one launch (start us, length us, event | category | flops | bytes accessed | tf_op | source)
XLA Modules:
  0.0 875.6 jit_solution(6989159653381708907)
XLA Ops:
  6.5 0.9 multiply_reduce_fusion
  7.4 9.3 %psum.84 = f32[10]{0:T(128)S(1)} all-reduce(f32[10]{0:T(128)S(1)} %get-tuple-element.8), channel_id=1, replica_groups=mesh['tm_0'=4,'tm_1'=4,'tm_2'=4,'tm_3'=2] {'tm_0'}, use_global_device_ids=true, to_apply=%region_1.0 | all-reduce | flops 10 | bytes 80 | tf_op jit(solution)/shard_map/psum | solution.py:14
  16.7 9.7 %psum.85 = f32[10]{0:T(128)S(1)} all-reduce(f32[10]{0:T(128)S(1)} %psum.84), channel_id=1, replica_groups=mesh['tm_0'=4,'tm_1'=4,'tm_2'=4,'tm_3'=2] {'tm_1'}, use_global_device_ids=true, to_apply=%region_2.0 | all-reduce | flops 10 | bytes 80 | tf_op jit(solution)/shard_map/psum | solution.py:14
  26.4 8.7 psum.86
  35.1 8.8 %psum.87 = f32[10]{0:T(128)S(1)} all-reduce(f32[10]{0:T(128)S(1)} %psum.86), channel_id=1, replica_groups=mesh['tm_0'=4,'tm_1'=4,'tm_2'=4,'tm_3'=2] {'tm_3'}, use_global_device_ids=true, to_apply=%region_4.0 | all-reduce | flops 10 | bytes 80 | tf_op jit(solution)/shard_map/psum | solution.py:14
  44.0 0.8 subtract_convert_fusion
  44.9 1.9 collective-permute-start.1
  46.8 2.4 collective-permute-start
  49.2 4.1 convert_reduce_fusion
  56.6 0.8 constant_dynamic-update-slice_fusion.44
  61.5 14.1 %convolution_bitcast_fusion = f32[8192,750]{0,1:T(8,128)} fusion(bf16[336,750]{0,1:T(8,128)(2,1)S(1)} %reshape.99, bf16[336,8192]{1,0:T(8,128)(2,1)} %param.5), kind=kOutput, calls=%fused_computation.3 | convolution fusion | flops 4128768000 | bytes 30585024 | tf_op jit(solution)/shard_map/dot_general | solution.py:85
  75.6 25.6 %reshape.100 = f32[8192,75,10]{0,2,1:T(8,128)} reshape(f32[8192,750]{0,1:T(8,128)} %convolution_bitcast_fusion) | data formatting | bytes 49152000 | tf_op jit(solution)/shard_map/reshape | solution.py:48
  101.2 37.2 %fusion.2 = f32[8192,10,61]{0,2,1:T(8,128)} fusion(f32[8192,75,10]{0,2,1:T(8,128)} %reshape.100, s32[10,61]{1,0:T(8,128)S(1)} %add_add_fusion), kind=kOutput, calls=%fused_computation.4 | convolution fusion | flops 4497453568 | bytes 44566920 | tf_op jit(solution)/shard_map/cjk,kjl->ckl/dot_general | solution.py:49
  138.4 17.9 %reshape.101 = f32[8192,610]{0,1:T(8,128)} reshape(f32[8192,10,61]{0,2,1:T(8,128)} %fusion.2) | data formatting | bytes 39976960 | tf_op jit(solution)/shard_map/reshape | solution.py:50
  156.3 15.2 %pad_maximum_fusion = f32[8192,612]{0,1:T(8,128)} fusion(f32[8192,1]{0,1:T(1,128)S(1)} %bitcast.334, f32[8192,1]{0,1:T(1,128)S(1)} %bitcast.333, f32[8192,610]{0,1:T(8,128)} %reshape.101), kind=kLoop, calls=%fused_computation.2 | loop fusion | flops 10027008 | bytes 40108032 | tf_op jit(solution)/shard_map/concatenate | solution.py:90
  171.5 22.0 %copy.13 = f32[8192,612]{1,0:T(8,128)} copy(f32[8192,612]{0,1:T(8,128)} %pad_maximum_fusion) | data formatting | bytes 40108032
  195.1 6.1 all-reduce.2
  201.2 6.1 all-reduce.1
  207.3 13.7 %all-reduce = (f32[10]{0:T(128)S(1)}, f32[610]{0:T(1024)S(1)}) all-reduce(f32[10]{0:T(128)S(1)} %get-tuple-element.11, f32[610]{0:T(1024)S(1)} %get-tuple-element.12), channel_id=1, replica_groups=mesh['tm_0'=4,'tm_1'=4,'tm_2'=4,'tm_3'=2] {'tm_2'}, use_global_device_ids=true, to_apply=%region_16.0 | all-reduce | flops 620 | bytes 4960 | tf_op jit(solution)/shard_map/psum | solution.py:14
  221.1 5.3 all-reduce.3
  226.4 639.1 %reduce-scatter.4.cloned.1.call-done = f32[64,612]{1,0:T(8,128)} async-done(((f32[8192,612]{1,0:T(8,128)}), f32[64,612]{1,0:T(8,128)}) %reduce-scatter.4.cloned.1.call-update) | async-done | bytes 156688
  865.5 0.9 slice_multiply_fusion.1
  866.5 1.1 copy.15
  867.9 0.9 copy.10
  (98 shorter events, 9.4 us)
Async XLA Ops:
  6.5 858.9 %reduce-scatter.4.cloned.1.call-start = ((), (), s32[]{:S(2)}) async-start(), calls=%async_computation.1 | async-start | bytes 21135360
  44.9 12.6 %collective-permute-start.1 = (bf16[44,10]{0,1:T(8,128)(2,1)S(1)}, bf16[44,10]{0,1:T(8,128)(2,1)S(1)}, u32[]{:S(2)}, u32[]{:S(2)}) collective-permute-start(bf16[44,10]{0,1:T(8,128)(2,1)S(1)} %get-tuple-element.19), channel_id=1, source_target_pairs={{0,1},{1,2},{2,3},{3,4},{4,5},{5,6},{6,7},{7,8},{8,9},{9,10},{10,1... | collective-permute-start | bytes 2648 | tf_op jit(solution)/shard_map/ppermute | solution.py:25
  46.8 7.3 collective-permute-start
  193.6 0.7 copy-start
Sparse Core Ops, SparseCore 0:
  193.7 671.7 reduce-scatter.3
where the time goes:
time: 884 us; the launch traced here: 876 us
  waiting for transfers between devices  639 us (72%)
  local copies, waits for them, and re-layouts  69 us (8%)
  blocking collectives  67.8 us (8%)
  matrix products  51.7 us (6%)
  other arithmetic  30.2 us (3%)
  between operations  13.5 us (2%)
    unnamed x2, waiting for transfers between devices  639 us
    psum x8, blocking collectives, one_axis_at_a_time(): array = lax.psum(array, axis)  67.8 us
    dot_general x2, matrix products, pick_lags(): jnp.einsum('cjk,kjl->ckl', spread, selector, precision=lax.Precision.HIGH...  37.6 us
    reshape x1, local copies, waits for them, and re-layouts, pick_lags(): spread = accum.reshape(accum.shape[0], count, kcount)  25.6 us
    unnamed x6, local copies, waits for them, and re-layouts  23.9 us
    reshape x1, local copies, waits for them, and re-layouts, pick_lags(): return chosen.reshape(accum.shape[0], kcount * lcount)  17.9 us
  transfers between devices with their start and end apart: 3, of which 1 were waited for; matrix products, arithmetic and copies ran while one was open for 1% of the time, Pallas kernels for 0%

commit v1 on v0

v1 whole, which is shorter than its diff:
```python
import functools

import jax
import jax.numpy as jnp
from jax import lax
from jax.experimental import pallas as pl
from jax.experimental.pallas import tpu as pltpu
from jax.sharding import Mesh
from jax.sharding import PartitionSpec as P

MAXLAG = 30
MAXOFF = 14
CHIPS = ("tm_0", "tm_1", "tm_2")
CORE = "tm_3"
TM = CHIPS + (CORE,)
PHASES = 6
LANES = 128
HALF = 64


def pack_kernel(field_ref, index_ref, order_ref, out_ref, index_rows):
    t_dev, kcount = index_ref.shape
    count = t_dev // PHASES
    order = order_ref[...]

    @pl.when(pl.program_id(0) == 0)
    def _():
        value = index_ref[...]
        upper = value.astype(jnp.bfloat16)
        lower = (value - upper.astype(jnp.float32)).astype(jnp.bfloat16)
        rows = []
        for part in (upper, lower):
            sorted_part = jnp.dot(order, part, preferred_element_type=jnp.float32)
            rows.extend(sorted_part[r * count : (r + 1) * count] for r in range(PHASES))
            rows.append(jnp.zeros((count, HALF - PHASES * kcount), jnp.float32))
        index_rows[...] = jnp.concatenate(rows, axis=1).astype(jnp.bfloat16)

    for chip in range(out_ref.shape[0]):
        block = field_ref[:, chip * LANES : (chip + 1) * LANES]
        sorted_block = jnp.dot(order, block, preferred_element_type=jnp.float32)
        out_ref[chip, 0:t_dev, :] = sorted_block.astype(jnp.bfloat16)
        out_ref[chip, t_dev:, :] = index_rows[...]


def pack(field, index):
    t_dev, cells = field.shape
    chips = cells // LANES
    count = t_dev // PHASES
    step = 8
    row = jnp.arange(t_dev)
    day = (row % count) * PHASES + row // count
    order = (day[:, None] == jnp.arange(t_dev)[None, :]).astype(jnp.bfloat16)
    return pl.pallas_call(
        pack_kernel,
        grid=(chips // step,),
        in_specs=[
            pl.BlockSpec((t_dev, step * LANES), lambda i: (0, i)),
            pl.BlockSpec(index.shape, lambda i: (0, 0)),
            pl.BlockSpec((t_dev, t_dev), lambda i: (0, 0)),
        ],
        out_specs=pl.BlockSpec((step, t_dev + count, LANES), lambda i: (i, 0, 0)),
        out_shape=jax.ShapeDtypeStruct((chips, t_dev + count, LANES), jnp.bfloat16),
        scratch_shapes=[pltpu.VMEM((count, LANES), jnp.bfloat16)],
    )(field, index, order)


def shards(field, index, lag_list, index_offset, sea_mask):
    t_dev, kcount = index.shape
    count = t_dev // PHASES
    chips = field.shape[1] // LANES
    total_days = t_dev * lax.axis_size(TM) * 1.0
    core = lax.axis_index(CORE)
    swap = [(0, 1), (1, 0)]
    used = PHASES * kcount

    sent = pack(field, index)
    got = lax.all_to_all(sent, CHIPS, 0, 0, tiled=True)
    days = got[:, :t_dev].reshape(chips, PHASES, count, LANES)
    own_raw = got[:, t_dev:]
    other_raw = lax.ppermute(own_raw, CORE, swap)

    def joined(raw):
        return (raw[..., :HALF].astype(jnp.float32) + raw[..., HALF:].astype(jnp.float32))[..., :used]

    own, other = joined(own_raw), joined(other_raw)
    first = (jnp.sum(own, (0, 1)) + jnp.sum(other, (0, 1))).reshape(PHASES, kcount).sum(0)
    second = (jnp.sum(own * own, (0, 1)) + jnp.sum(other * other, (0, 1))).reshape(PHASES, kcount).sum(0)
    mean_i = first / total_days
    var_i = second / total_days - mean_i * mean_i
    mean_row = jnp.tile(mean_i, PHASES)
    own = (own - mean_row).astype(jnp.bfloat16)
    other = (other - mean_row).astype(jnp.bfloat16)
    edge = jnp.pad(other, ((1, 1), (0, 0), (0, 0)))
    before = lax.dynamic_slice_in_dim(edge, core, chips, 0)[:, count - 8 :]
    after = lax.dynamic_slice_in_dim(edge, core + 1, chips, 0)[:, :8]
    extended = jnp.concatenate([before, own, after], 1)
    windows = jnp.concatenate([extended[:, m : m + count] for m in range(14)], 2)
    spread = jnp.einsum("irbc,ibw->rcw", days, windows, preferred_element_type=jnp.float32)
    spread = spread.reshape(PHASES, LANES, 14 * PHASES, kcount)
    window_sums = jnp.sum(windows.astype(jnp.float32), (0, 1)).reshape(14 * PHASES, kcount)
    lags_all = MAXLAG + MAXLAG + MAXOFF + 1
    accum = sum(spread[r, :, 4 + r : 4 + r + lags_all] for r in range(PHASES))
    totals = sum(window_sums[4 + r : 4 + r + lags_all] for r in range(PHASES))
    wide = days.astype(jnp.float32)
    first_sum = jnp.sum(wide, (0, 1, 2))
    second_sum = jnp.sum(wide * wide, (0, 1, 2))

    def swapped(mine):
        halves = mine.reshape(2, HALF, *mine.shape[1:])
        kept = lax.dynamic_index_in_dim(halves, core, 0, keepdims=False)
        passed = lax.dynamic_index_in_dim(halves, 1 - core, 0, keepdims=False)
        return kept + lax.ppermute(passed, CORE, swap)

    accum = swapped(accum)
    sums = swapped(jnp.stack([first_sum, second_sum], 1))
    totals = totals + lax.ppermute(totals, CORE, swap)
    shifts = lag_list[None, :] + index_offset[:, None]
    place = MAXLAG + MAXOFF - shifts
    selector = (jnp.arange(lags_all)[None, :, None] == place[:, None, :]).astype(jnp.float32)
    products = jnp.einsum("cjk,kjl->ckl", accum, selector, precision=lax.Precision.HIGHEST)
    prefix_totals = jnp.einsum("jk,kjl->kl", totals, selector, precision=lax.Precision.HIGHEST)
    mean_x = sums[:, 0] / total_days
    var_x = sums[:, 1] / total_days - mean_x * mean_x
    numer = products - mean_x[:, None, None] * prefix_totals[None]
    scale = (
        total_days * jnp.sqrt(var_x + 1e-06)[:, None, None] * jnp.sqrt(var_i + 1e-06)[None, :, None]
    )
    return numer / scale * sea_mask.astype(jnp.float32)[:, None, None]


def solution(mesh):
    finer = Mesh(mesh.devices.reshape(4, 4, 4, 2), TM)
    return jax.shard_map(
        shards,
        mesh=finer,
        in_specs=(P(TM, None), P(TM, None), P(), P(), P(TM)),
        out_specs=P(TM, None, None),
        check_vma=False,
    )
```

time: 884 us -> 219 us (0.25)
  the two profiles are of different devices: /device:TPU:1 before, /device:TPU:103 now
where the time goes in v1:
time: 219 us; the launch traced here: 217 us
  waiting for transfers between devices  92.4 us (42%)
  local copies, waits for them, and re-layouts  70.8 us (32%)
  other arithmetic  19.8 us (9%)
  starting transfers between devices  11.6 us (5%)
  Pallas kernels  11.4 us (5%)
  matrix products  10.4 us (5%)
    all_to_all x1, waiting for transfers between devices, shards(): got = lax.all_to_all(sent, CHIPS, 0, 0, tiled=True)  91.3 us
    dot_general x2, local copies, waits for them, and re-layouts, shards(): jnp.einsum('irbc,ibw->rcw', days, windows, preferred_element_type=jnp.flo...  41.7 us
    concatenate x1, local copies, waits for them, and re-layouts, shards(): windows = jnp.concatenate([extended[:, m:m + count] for m in range(14)], 2)  15 us
    pallas_call x1, Pallas kernels, pack(): pl.pallas_call(pack_kernel, grid=(chips // step,), in_specs=[pl.BlockSpec...  11.4 us
    all_to_all x1, starting transfers between devices, shards(): got = lax.all_to_all(sent, CHIPS, 0, 0, tiled=True)  10.1 us
    dot_general x1, matrix products, shards(): jnp.einsum('irbc,ibw->rcw', days, windows, preferred_element_type=jnp.flo...  9.5 us
    concatenate x2, other arithmetic, shards(): extended = jnp.concatenate([before, own, after], 1)  6.23 us
    reduce_sum x1, other arithmetic, shards(): second_sum = jnp.sum(wide * wide, (0, 1, 2))  5.41 us
  transfers between devices with their start and end apart: 5, of which 2 were waited for; matrix products, arithmetic and copies ran while one was open for 28% of the time, Pallas kernels for 0%

profile of v1, /device:TPU:103, one launch (start us, length us, event | category | flops | bytes accessed | tf_op | source)
XLA Modules:
  0.0 216.6 jit_solution(7136205651052364524)
XLA Ops:
  0.0 1.5 copy.17.index_ref
  1.5 0.8 fusion.25.order_ref
  2.4 11.4 %shard_map.55 = bf16[64,392,128]{2,1,0:T(8,128)(2,1)} custom-call(bf16[336,8192]{1,0:T(8,128)(2,1)} %field_ref.1, f32[336,10]{1,0:T(8,128)} %copy.17.index_ref, bf16[336,336]{1,0:T(8,128)(2,1)} %fusion.25.order_ref), custom_call_target="tpu_custom_call" | custom-call | tf_op jit(solution)/shard_map/pallas_call | solution.py:53
  13.8 10.1 %all-to-all-start = ((bf16[64,392,128]{2,1,0:T(8,128)(2,1)}), bf16[64,392,128]{2,1,0:T(8,128)(2,1)}, u32[]{:S(2)}, u32[]{:S(2)}) async-start(bf16[64,392,128]{2,1,0:T(8,128)(2,1)} %shard_map.55), calls=%async_computation | async-start | bytes 12845056 | tf_op jit(solution)/shard_map/all_to_all | solution.py:77
  24.0 91.3 %all-to-all-done = bf16[64,392,128]{2,1,0:T(8,128)(2,1)} async-done(((bf16[64,392,128]{2,1,0:T(8,128)(2,1)}), bf16[64,392,128]{2,1,0:T(8,128)(2,1)}, u32[]{:S(2)}, u32[]{:S(2)}) %all-to-all-start) | async-done | bytes 6422560 | tf_op jit(solution)/shard_map/all_to_all | solution.py:77
  115.3 5.4 %fusion = (f32[128]{0:T(128)S(1)}, f32[128]{0:T(128)S(1)}) fusion(bf16[64,392,128]{2,1,0:T(8,128)(2,1)} %all-to-all-done), kind=kLoop, calls=%fused_computation.3 | loop fusion | flops 11009792 | bytes 5506048 | tf_op jit(solution)/shard_map/reduce_sum | solution.py:106
  120.9 1.3 slice.221
  122.2 0.6 collective-permute-start
  122.9 2.0 fusion.41
  124.9 5.3 %slice.220 = bf16[64,336,128]{2,1,0:T(8,128)(2,1)} slice(bf16[64,392,128]{2,1,0:T(8,128)(2,1)} %all-to-all-done), slice={[0:64], [0:336], [0:128]} | slice | bytes 11010048 | tf_op jit(solution)/shard_map/slice | solution.py:78
  130.6 1.0 multiply_reduce_fusion
  132.2 2.1 subtract_convert_fusion
  134.3 2.6 %pad_maximum_fusion = (bf16[64,56,60]{2,1,0:T(8,128)(2,1)S(1)}, bf16[64,56,60]{2,1,0:T(8,128)(2,1)S(1)}, bf16[64,56,60]{2,1,0:T(8,128)(2,1)}, bf16[64,56,60]{2,1,0:T(8,128)(2,1)}, bf16[64,56,60]{2,1,0:T(8,128)(2,1)}) fusion(bf16[64,8,60]{2,1,0:T(8,128)(2,1)S(1)} %get-tuple-element.26, bf16[64,56,60]{2,1,0:T(8,128)(2,1)S(1)} %get-tuple-element.36), kind=kLoop, calls=%fused_computation.42 | loop fusion | flops 4300800 | bytes 2641920 | tf_op jit(solution)/shard_map/concatenate | solution.py:96
  136.9 3.7 %pad_maximum_fusion.1 = (bf16[64,56,60]{2,1,0:T(8,128)(2,1)}, bf16[64,56,60]{2,1,0:T(8,128)(2,1)}, bf16[64,56,60]{2,1,0:T(8,128)(2,1)}, bf16[64,56,60]{2,1,0:T(8...) fusion(bf16[64,56,60]{2,1,0:T(8,128)(2,1)S(1)} %get-tuple-eleme, ...), kind=kLoop, calls=%fused_computation.43 | loop fusion | flops 6881280 | bytes 3932160 | tf_op jit(solution)/shard_map/concatenate | solution.py:96
  140.5 15.0 %concatenate.24 = bf16[64,56,840]{2,1,0:T(8,128)(2,1)} concatenate(bf16[64,56,60]{2,1,0:T(8,128)(2,1)} %get-tuple-element.19, bf16[64,56,60]{2,1,0:T(8,128)(2,1)} %get-tuple-element.20, bf16[64,56,60]{2,1,0:T(8,128)(2,1)} %get-tuple-element.21, bf16[64,56,60]{2,1,0:T(8,128)(2,1)} %get-tuple-element.22, bf16[64,56,60]{2,1,0:T(8,128)(2,1)} %get-tuple-element.23, ...), dimensions={2} | concatenate | bytes 12042240 | tf_op jit(solution)/shard_map/concatenate | solution.py:97
  155.5 3.8 %convert_reduce_fusion.1 = f32[840]{0:T(1024)S(1)} fusion(bf16[64,56,840]{2,1,0:T(8,128)(2,1)} %concatenate.24), kind=kLoop, calls=%fused_computation.2 | loop fusion | flops 6020280 | bytes 6024480 | tf_op jit(solution)/shard_map/reduce_sum | solution.py:100
  159.5 0.7 collective-permute-start.3
  160.3 25.7 %copy.18 = bf16[840,56,64]{2,1,0:T(8,128)(2,1)} copy(bf16[840,56,64]{0,1,2:T(8,128)(2,1)} %bitcast.47) | data formatting | bytes 12042240 | tf_op jit(solution)/shard_map/irbc,ibw->rcw/dot_general | solution.py:98
  186.0 15.9 %copy.20 = bf16[84,10,56,64]{0,2,3,1:T(8,128)(2,1)} copy(bf16[84,10,56,64]{3,2,1,0:T(8,128)(2,1)} %bitcast.48) | data formatting | bytes 12042240 | tf_op jit(solution)/shard_map/irbc,ibw->rcw/dot_general | solution.py:98
  201.9 9.5 %fusion.4 = f32[6,128,84,10]{1,2,3,0:T(8,128)S(1)} fusion(bf16[84,10,56,64]{0,2,3,1:T(8,128)(2,1)} %copy.20, bf16[64,6,56,128,1]{3,2,1,0,4:T(8,128)(2,1)} %bitcast.49), kind=kOutput, calls=%fused_computation.24 | convolution fusion | flops 4624220160 | bytes 14106624 | tf_op jit(solution)/shard_map/irbc,ibw->rcw/dot_general | solution.py:98
  211.7 0.4 reshape.203
  212.2 0.7 constant_dynamic-slice_fusion.3
  214.2 1.1 collective-permute-done.1
  215.7 0.9 copy.23
  (48 shorter events, 3.6 us)
Async XLA Ops:
  13.7 10.1 %copy-start.4 = (s32[64]{0:T(128)S(1)}, s32[64]{0:T(128)}, u32[]{:S(2)}) copy-start(s32[64]{0:T(128)} %param.9) | copy-start | bytes 772
  13.7 10.2 %copy-start.2 = (s32[10]{0:T(128)S(1)}, s32[10]{0:T(128)}, u32[]{:S(2)}) copy-start(s32[10]{0:T(128)} %param.8) | copy-start | bytes 124
  13.7 10.2 %copy-start.3 = (s32[61]{0:T(128)S(1)}, s32[61]{0:T(128)}, u32[]{:S(2)}) copy-start(s32[61]{0:T(128)} %param.7) | copy-start | bytes 736
  13.8 101.6 %all-to-all-start = ((bf16[64,392,128]{2,1,0:T(8,128)(2,1)}), bf16[64,392,128]{2,1,0:T(8,128)(2,1)}, u32[]{:S(2)}, u32[]{:S(2)}) async-start(bf16[64,392,128]{2,1,0:T(8,128)(2,1)} %shard_map.55), calls=%async_computation | async-start | bytes 12845056 | tf_op jit(solution)/shard_map/all_to_all | solution.py:77
  122.2 8.1 %collective-permute-start = (bf16[64,56,128]{2,1,0:T(8,128)(2,1)S(1)}, bf16[64,56,128]{2,1,0:T(8,128)(2,1)S(1)}, u32[]{:S(2)}, u32[]{:S(2)}) collective-permute-start(bf16[64,56,128]{2,1,0:T(8,128)(2,1)S(1)} %slice.221), channel_id=1, source_target_pairs={{0,1},{1,0},{2,3},{3,2},{4,5},{5,4},{6,7},{7,6},{8,9},{9,8},{10,11... | collective-permute-start | bytes 2752520 | tf_op jit(solution)/shard_map/ppermute | solution.py:80
  122.7 7.5 %collective-permute-start.2 = (f32[64,2]{0,1:T(2,128)S(1)}, f32[64,2]{0,1:T(2,128)S(1)}, u32[]{:S(2)}, u32[]{:S(2)}) collective-permute-start(f32[64,2]{0,1:T(2,128)S(1)} %bitcast.53), channel_id=1, source_target_pairs={{0,1},{1,0},{2,3},{3,2},{4,5},{5,4},{6,7},{7,6},{8,9},{9,8},{10,11... | collective-permute-start | bytes 1544 | tf_op jit(solution)/shard_map/ppermute | solution.py:112
  130.6 1.0 copy-start
  130.6 1.2 copy-start.1
  159.5 54.1 %collective-permute-start.3 = (f32[75,10]{1,0:T(8,128)S(1)}, f32[75,10]{1,0:T(8,128)S(1)}, u32[]{:S(2)}, u32[]{:S(2)}) collective-permute-start(f32[75,10]{1,0:T(8,128)S(1)} %reshape.204), channel_id=1, source_target_pairs={{0,1},{1,0},{2,3},{3,2},{4,5},{5,4},{6,7},{7,6},{8,9},{9,8},{10,11... | collective-permute-start | bytes 9008 | tf_op jit(solution)/shard_map/ppermute | solution.py:116
  213.5 1.7 collective-permute-start.1

commit v2 on v1

v2 whole, which is shorter than its diff:
```python
import jax
import jax.numpy as jnp
from jax import lax
from jax.experimental import pallas as pl
from jax.experimental.pallas import tpu as pltpu
from jax.sharding import Mesh
from jax.sharding import PartitionSpec as P

MAXLAG = 30
MAXOFF = 14
CHIPS = ("tm_0", "tm_1", "tm_2")
CORE = "tm_3"
TM = CHIPS + (CORE,)
PHASES = 6
LANES = 128
HALF = 64
BEFORE = 8
TILES = 7
WIDTH = TILES * LANES
SUM_LANE = BEFORE * HALF + 60
SQUARE_LANE = SUM_LANE + 1
ROWS = HALF + 8
F32 = jnp.float32
BF16 = jnp.bfloat16


def pack_kernel(field_ref, index_ref, order_ref, out_ref, index_rows):
    t_dev, kcount = index_ref.shape
    count = t_dev // PHASES
    order = order_ref[...]

    @pl.when(pl.program_id(0) == 0)
    def _():
        value = index_ref[...]
        upper = value.astype(BF16)
        lower = (value - upper.astype(F32)).astype(BF16)
        rows = []
        for part in (upper, lower):
            sorted_part = jnp.dot(order, part, preferred_element_type=F32)
            rows.extend(sorted_part[r * count : (r + 1) * count] for r in range(PHASES))
            rows.append(jnp.zeros((count, HALF - PHASES * kcount), F32))
        index_rows[...] = jnp.concatenate(rows, axis=1).astype(BF16)

    for pair in range(out_ref.shape[0] // 2):
        block = field_ref[:, pair * 2 * LANES : (pair + 1) * 2 * LANES]
        sorted_block = jnp.dot(order, block, preferred_element_type=F32).astype(BF16)
        out_ref[2 * pair, 0:t_dev, :] = sorted_block[:, :LANES]
        out_ref[2 * pair + 1, 0:t_dev, :] = sorted_block[:, LANES:]
        out_ref[2 * pair, t_dev:, :] = index_rows[...]
        out_ref[2 * pair + 1, t_dev:, :] = index_rows[...]


def pack(field, index):
    t_dev, cells = field.shape
    chips = cells // LANES
    count = t_dev // PHASES
    step = 8
    row = jnp.arange(t_dev)
    day = (row % count) * PHASES + row // count
    order = (day[:, None] == jnp.arange(t_dev)[None, :]).astype(BF16)
    return pl.pallas_call(
        pack_kernel,
        grid=(chips // step,),
        in_specs=[
            pl.BlockSpec((t_dev, step * LANES), lambda i: (0, i)),
            pl.BlockSpec(index.shape, lambda i: (0, 0)),
            pl.BlockSpec((t_dev, t_dev), lambda i: (0, 0)),
        ],
        out_specs=pl.BlockSpec((step, t_dev + count, LANES), lambda i: (i, 0, 0)),
        out_shape=jax.ShapeDtypeStruct((chips, t_dev + count, LANES), BF16),
        scratch_shapes=[pltpu.VMEM((count, LANES), BF16)],
    )(field, index, order)


def square_kernel(got_ref, out_ref):
    @pl.when(pl.program_id(0) == 0)
    def _():
        out_ref[...] = jnp.zeros_like(out_ref)

    wide = got_ref[...].astype(F32)
    groups = (wide * wide).reshape(-1, 8, LANES)
    out_ref[...] += jnp.sum(groups, 0)


def squares(got, t_dev):
    chips = got.shape[0]
    step = 8
    return pl.pallas_call(
        square_kernel,
        grid=(chips // step,),
        in_specs=[pl.BlockSpec((step, t_dev, LANES), lambda i: (i, 0, 0))],
        out_specs=pl.BlockSpec((8, LANES), lambda i: (0, 0)),
        out_shape=jax.ShapeDtypeStruct((8, LANES), F32),
    )(got)


def joined(raw):
    wide = raw.astype(F32)
    return wide + pltpu.roll(wide, HALF, 2)


def shifted(parts):
    total = parts[0]
    lane = lax.broadcasted_iota(jnp.int32, total.shape, 1) % HALF
    for r in range(1, PHASES):
        near = pltpu.roll(parts[r], WIDTH - 10 * r, 1)
        far = pltpu.roll(parts[r], WIDTH - 10 * r - 4, 1)
        total = total + jnp.where(lane + 10 * r < 60, near, far)
    return total


def spread_kernel(
    core_ref, own_ref, other_ref, square_ref, got_ref,
    kept_ref, passed_ref, stat_ref,
    days, edge, ext, win, acc, sems,
):
    chips, count, _ = own_ref.shape
    core = core_ref[0]
    copies = []
    for r in range(PHASES):
        copy = pltpu.make_async_copy(
            got_ref.at[:, r * count : (r + 1) * count, :], days.at[r], sems.at[r]
        )
        copy.start()
        copies.append(copy)

    total_days = 2.0 * chips * count * PHASES
    own = joined(own_ref[...])
    other = joined(other_ref[...])
    first = jnp.sum(own, (0, 1), keepdims=True)[0] + jnp.sum(other, (0, 1), keepdims=True)[0]
    second = (
        jnp.sum(own * own, (0, 1), keepdims=True)[0]
        + jnp.sum(other * other, (0, 1), keepdims=True)[0]
    )
    row = lax.broadcasted_iota(jnp.int32, (LANES, LANES), 0)
    column = lax.broadcasted_iota(jnp.int32, (LANES, LANES), 1) % HALF
    same = (row < 60) & (column < 60) & (row % 10 == column % 10)
    sums = jnp.concatenate([first, second, jnp.zeros((6, LANES), F32)], 0)
    folded = jnp.dot(
        sums, same.astype(F32), precision=lax.Precision.HIGHEST, preferred_element_type=F32
    )
    mean = folded[0:1] / total_days
    var = folded[1:2] / total_days - mean * mean
    stat_ref[...] = jnp.concatenate([mean, var, jnp.zeros((6, LANES), F32)], 0)
    lane = lax.broadcasted_iota(jnp.int32, (1, 1, LANES), 2)
    valid = lane % HALF < 60

    def centered(value):
        return jnp.where(valid, (value - mean[None]).astype(BF16).astype(F32), 0.0)

    own = centered(own)
    other = centered(other)
    zero = jnp.zeros((1, 16, LANES), F32)
    edge[0:1] = zero
    edge[chips + 1 : chips + 2] = zero
    edge[1 : chips + 1, 0:8, :] = other[:, 0:8, :]
    edge[1 : chips + 1, 8:16, :] = other[:, count - 8 :, :]
    ext[:, 0:8, :] = edge[pl.ds(core, chips), 8:16, :]
    ext[:, 8 : 8 + count, :] = jnp.where(lane == 60, 1.0, own)
    ext[:, 8 + count :, :] = edge[pl.ds(core + 1, chips), 0:8, :]
    window_sums = []
    for q in range(TILES):
        tile = jnp.where(
            lane < HALF,
            ext[:, 2 * q : 2 * q + count, :],
            ext[:, 2 * q + 1 : 2 * q + 1 + count, :],
        )
        window_sums.append(jnp.sum(tile, (0, 1), keepdims=True)[0])
        tile = tile.astype(BF16)
        for chip in range(chips):
            win[chip * count : (chip + 1) * count, q * LANES : (q + 1) * LANES] = tile[chip]
    for copy in copies:
        copy.wait()
    for r in range(PHASES):
        flat = days.at[r].reshape(chips * count, LANES)[...]
        acc[r * LANES : (r + 1) * LANES, :] = lax.dot_general(
            flat, win[...], (((0,), (0,)), ((), ())), preferred_element_type=F32
        )
    parts = [acc[r * LANES : (r + 1) * LANES, :] for r in range(PHASES)]
    result = shifted(parts)
    plain = sum(parts)
    squared = jnp.sum(square_ref[...], 0, keepdims=True)
    square_column = jnp.transpose(jnp.broadcast_to(squared, (LANES, LANES)))[:, 0:1]
    lanes = lax.broadcasted_iota(jnp.int32, result.shape, 1)
    result = jnp.where(lanes == SUM_LANE, plain, result)
    result = jnp.where(lanes == SQUARE_LANE, square_column, result)
    acc[0:LANES, :] = result
    sums_row = jnp.broadcast_to(jnp.concatenate(window_sums, 1), (8, WIDTH))
    totals = shifted([sums_row] * PHASES)
    kept_ref[0:HALF, :] = acc[pl.ds(pl.multiple_of(core * HALF, HALF), HALF), :]
    passed_ref[0:HALF, :] = acc[pl.ds(pl.multiple_of((1 - core) * HALF, HALF), HALF), :]
    kept_ref[HALF:, :] = totals
    passed_ref[HALF:, :] = totals


def spread(core, own, other, square, got):
    chips, count, _ = own.shape
    vmem = pl.BlockSpec(memory_space=pltpu.VMEM)
    half = jax.ShapeDtypeStruct((ROWS, WIDTH), F32)
    return pl.pallas_call(
        spread_kernel,
        in_specs=[pl.BlockSpec(memory_space=pltpu.SMEM), vmem, vmem, vmem, pl.BlockSpec(memory_space=pl.ANY)],
        out_specs=[vmem] * 3,
        out_shape=[half, half, jax.ShapeDtypeStruct((8, LANES), F32)],
        scratch_shapes=[
            pltpu.VMEM((PHASES, chips, count, LANES), BF16),
            pltpu.VMEM((chips + 2, 16, LANES), F32),
            pltpu.VMEM((chips, count + 16, LANES), F32),
            pltpu.VMEM((chips * count, WIDTH), BF16),
            pltpu.VMEM((PHASES * LANES, WIDTH), F32),
            pltpu.SemaphoreType.DMA((PHASES,)),
        ],
        compiler_params=pltpu.CompilerParams(vmem_limit_bytes=60 << 20),
    )(core, own, other, square, got)


def finish_kernel(kept_ref, taken_ref, stat_ref, place_ref, mask_ref, days_ref, out_ref):
    total_days = days_ref[0]
    value = kept_ref[...] + taken_ref[...]
    upper = value.astype(BF16)
    rest = value - upper.astype(F32)
    middle = rest.astype(BF16)
    lower = (rest - middle.astype(F32)).astype(BF16)
    mean_x = value[0:HALF, SUM_LANE : SUM_LANE + 1] / total_days
    var_x = value[0:HALF, SQUARE_LANE : SQUARE_LANE + 1] / total_days - mean_x * mean_x
    scale_x = total_days * jnp.sqrt(var_x + 1e-06)
    scale_i = jnp.sqrt(stat_ref[1:2, :] + 1e-06)
    mask = mask_ref[...].astype(F32)
    row = lax.broadcasted_iota(jnp.int32, (WIDTH, LANES), 0)
    for k in range(out_ref.shape[1]):
        selector = (row == place_ref[k : k + 1, :]).astype(BF16)
        chosen = (
            jnp.dot(upper, selector, preferred_element_type=F32)
            + jnp.dot(middle, selector, preferred_element_type=F32)
            + jnp.dot(lower, selector, preferred_element_type=F32)
        )
        numer = chosen[0:HALF] - mean_x * chosen[HALF : HALF + 1]
        answer = numer / (scale_x * scale_i[:, k : k + 1]) * mask
        out_ref[:, k, :] = answer[:, : out_ref.shape[2]]


def finish(kept, taken, stat, place, mask, total_days, lags):
    vmem = pl.BlockSpec(memory_space=pltpu.VMEM)
    kcount = place.shape[0]
    return pl.pallas_call(
        finish_kernel,
        in_specs=[vmem] * 5 + [pl.BlockSpec(memory_space=pltpu.SMEM)],
        out_specs=vmem,
        out_shape=jax.ShapeDtypeStruct((HALF, kcount, lags), F32),
    )(kept, taken, stat, place, mask, total_days)


def shards(field, index, lag_list, index_offset, sea_mask):
    t_dev, kcount = index.shape
    swap = [(0, 1), (1, 0)]
    total_days = jnp.full((1,), t_dev * lax.axis_size(TM), F32)
    core = lax.axis_index(CORE).astype(jnp.int32).reshape(1)
    got = lax.all_to_all(pack(field, index), CHIPS, 0, 0, tiled=True)
    own = got[:, t_dev:]
    other = lax.ppermute(own, CORE, swap)
    square = squares(got, t_dev)
    kept, passed, stat = spread(core, own, other, square, got)
    taken = lax.ppermute(passed, CORE, swap)
    shifts = lag_list[None, :] + index_offset[:, None]
    slot = BEFORE * PHASES - shifts
    place = HALF * (slot // PHASES) + kcount * (slot % PHASES) + jnp.arange(kcount)[:, None]
    place = jnp.pad(place, ((0, 0), (0, LANES - place.shape[1])), constant_values=-1)
    return finish(
        kept, taken, stat, place.astype(jnp.int32), sea_mask[:, None], total_days, lag_list.shape[0]
    )


def solution(mesh):
    finer = Mesh(mesh.devices.reshape(4, 4, 4, 2), TM)
    return jax.shard_map(
        shards,
        mesh=finer,
        in_specs=(P(TM, None), P(TM, None), P(), P(), P(TM)),
        out_specs=P(TM, None, None),
        check_vma=False,
    )
```

time: 219 us -> 137 us (0.63)
  the two profiles are of different devices: /device:TPU:103 before, /device:TPU:1 now
where the time goes in v2:
time: 137 us
  blocking collectives  90.3 us (66%)
  Pallas kernels  33.6 us (25%)
  local copies, waits for them, and re-layouts  9.13 us (7%)
  starting transfers between devices  2.53 us (2%)
    all_to_all x1, blocking collectives, shards(): got = lax.all_to_all(pack(field, index), CHIPS, 0, 0, tiled=True)  90.3 us
    pallas_call x1, Pallas kernels, spread(): pl.pallas_call(spread_kernel, in_specs=[pl.BlockSpec(memory_space=pltpu.S...  13.1 us
    pallas_call x1, Pallas kernels, pack(): pl.pallas_call(pack_kernel, grid=(chips // step,), in_specs=[pl.BlockSpec...  9.59 us
    pallas_call x1, Pallas kernels, squares(): pl.pallas_call(square_kernel, grid=(chips // step,), in_specs=[pl.BlockSp...  7 us
    unnamed x15, local copies, waits for them, and re-layouts  5.89 us
    pallas_call x1, Pallas kernels, finish(): pl.pallas_call(finish_kernel, in_specs=[vmem] * 5 + [pl.BlockSpec(memory_...  3.89 us
  transfers between devices with their start and end apart: 2, of which 1 were waited for; matrix products, arithmetic and copies ran while one was open for 1% of the time, Pallas kernels for 5%

profile of v2, /device:TPU:1, one launch (start us, length us, event | category | flops | bytes accessed | tf_op | source)
XLA Modules:
  0.0 136.7 jit_solution(1511517948228224843)
XLA Ops:
  0.0 0.8 fusion.order_ref
  0.8 1.5 %copy.6.index_ref = f32[336,10]{1,0:T(8,128)} copy(f32[336,10]{0,1:T(8,128)} %param.6) | data formatting | bytes 26880 | tf_op args[1]
  2.4 9.6 %shard_map.55 = bf16[64,392,128]{2,1,0:T(8,128)(2,1)} custom-call(bf16[336,8192]{1,0:T(8,128)(2,1)} %field_ref.1, f32[336,10]{1,0:T(8,128)} %copy.6.index_ref, bf16[336,336]{1,0:T(8,128)(2,1)} %fusion.order_ref), custom_call_target="tpu_custom_call" | custom-call | tf_op jit(solution)/shard_map/pallas_call | solution.py:61
  12.0 90.3 %all_to_all.5.got_ref = bf16[64,392,128]{2,1,0:T(8,128)(2,1)S(1)} all-to-all(bf16[64,392,128]{2,1,0:T(8,128)(2,1)} %shard_map.55), channel_id=1, replica_groups=mesh['tm_0'=4,'tm_1'=4,'tm_2'=4,'tm_3'=2] {'tm_0','tm_1','tm_2'}, dimensions={0} | all-to-all | bytes 12845056 | tf_op jit(solution)/shard_map/all_to_all | solution.py:258
  102.3 2.7 %copy-done = bf16[64,392,128]{2,1,0:T(8,128)(2,1)} copy-done((bf16[64,392,128]{2,1,0:T(8,128)(2,1)}, bf16[64,392,128]{2,1,0:T(8,128)(2,1)S(1)}, u32[]{:S(2)}) %copy-start) | copy-done | bytes 6422552
  105.0 0.1 slice.4.own_ref
  105.1 0.0 copy-start.1
  105.1 2.2 %collective-permute-start = (bf16[64,56,128]{2,1,0:T(8,128)(2,1)S(1)}, bf16[64,56,128]{2,1,0:T(8,128)(2,1)S(1)}, u32[]{:S(2)}, u32[]{:S(2)}) collective-permute-start(bf16[64,56,128]{2,1,0:T(8,128)(2,1)S(1)} %slice.4.own_ref), channel_id=1, source_target_pairs={{0,1},{1,0},{2,3},{3,2},{4,5},{5,4},{6,7},{7,6},{8,9},{9,8},{10,11... | collective-permute-start | bytes 2752520 | tf_op jit(solution)/shard_map/ppermute | solution.py:260
  107.3 7.0 %shard_map.56.square_ref = f32[8,128]{1,0:T(8,128)} custom-call(bf16[64,392,128]{2,1,0:T(8,128)(2,1)} %copy-done), custom_call_target="tpu_custom_call" | custom-call | tf_op jit(solution)/shard_map/pallas_call | solution.py:88
  114.3 0.0 collective-permute-done.other_ref
  114.3 0.0 copy-done.1
  114.3 0.9 copy-done.2
  115.2 13.1 %shard_map.57 = (f32[72,896]{1,0:T(8,128)}, f32[72,896]{1,0:T(8,128)}, f32[8,128]{1,0:T(8,128)}) custom-call(s32[1]{0:T(128)} %bitcast.core_ref, bf16[64,56,128]{2,1,0:T(8,128)(2,1)} %copy-done.1, bf16[64,56,128]{2,1,0:T(8,128)(2,1)} %copy-done.2, f32[8,128]{1,0:T(8,128)} %shard_map.56.square_ref, bf16[64,392,128]{2,1,0:T(8,128)(2,1)} %copy-done), custom_call_target="tpu_custom_call" | custom-call | tf_op jit(solution)/shard_map/pallas_call | solution.py:200
  128.4 0.3 collective-permute-start.1
  128.7 0.0 copy-done.4
  128.7 0.7 copy.7.mask_ref
  129.4 0.0 copy-done.5
  129.4 0.0 copy-done.6
  129.4 0.1 fusion.3
  129.5 0.6 pad.4.place_ref
  130.1 0.1 collective-permute-done.1.taken_ref
  130.2 0.7 copy-done.3
  130.9 3.9 %shard_map.58 = f32[64,10,61]{2,1,0:T(8,128)} custom-call(f32[72,896]{1,0:T(8,128)} %get-tuple-element.8.kept_ref, f32[72,896]{1,0:T(8,128)} %copy-done.3, f32[8,128]{1,0:T(8,128)} %get-tuple-element.10.stat_ref, s32[10,128]{1,0:T(8,128)} %pad.4.place_ref, s32[64,1]{1,0:T(8,128)} %copy.7.mask_ref, f32[1]{0:T(128)} %constant.50.clone.1.days_ref), custom_call_target="tpu_custom_call" | custom-call | tf_op jit(solution)/shard_map/pallas_call | solution.py:245
  134.8 1.9 %copy.8 = f32[64,10,61]{2,0,1:T(8,128)} copy(f32[64,10,61]{2,1,0:T(8,128)} %shard_map.58) | data formatting | bytes 312320 | tf_op jit(solution)/shard_map/pallas_call | solution.py:245
  (7 shorter events, 0.0 us)
Async XLA Ops:
  102.3 2.7 %copy-start = (bf16[64,392,128]{2,1,0:T(8,128)(2,1)}, bf16[64,392,128]{2,1,0:T(8,128)(2,1)S(1)}, u32[]{:S(2)}) copy-start(bf16[64,392,128]{2,1,0:T(8,128)(2,1)S(1)} %all_to_all.5.got_ref) | copy-start | bytes 19267588
  105.1 9.2 %copy-start.1 = (bf16[64,56,128]{2,1,0:T(8,128)(2,1)}, bf16[64,56,128]{2,1,0:T(8,128)(2,1)S(1)}, u32[]{:S(2)}) copy-start(bf16[64,56,128]{2,1,0:T(8,128)(2,1)S(1)} %slice.4.own_ref) | copy-start | bytes 2752516
  105.1 9.2 %collective-permute-start = (bf16[64,56,128]{2,1,0:T(8,128)(2,1)S(1)}, bf16[64,56,128]{2,1,0:T(8,128)(2,1)S(1)}, u32[]{:S(2)}, u32[]{:S(2)}) collective-permute-start(bf16[64,56,128]{2,1,0:T(8,128)(2,1)S(1)} %slice.4.own_ref), channel_id=1, source_target_pairs={{0,1},{1,0},{2,3},{3,2},{4,5},{5,4},{6,7},{7,6},{8,9},{9,8},{10,11... | collective-permute-start | bytes 2752520 | tf_op jit(solution)/shard_map/ppermute | solution.py:260
  107.3 21.4 %copy-start.4 = (s32[64]{0:T(128)S(1)}, s32[64]{0:T(128)}, u32[]{:S(2)}) copy-start(s32[64]{0:T(128)} %param.9) | copy-start | bytes 772
  107.3 22.1 %copy-start.5 = (s32[10]{0:T(128)S(1)}, s32[10]{0:T(128)}, u32[]{:S(2)}) copy-start(s32[10]{0:T(128)} %param.8) | copy-start | bytes 124
  107.3 22.1 %copy-start.6 = (s32[61]{0:T(128)S(1)}, s32[61]{0:T(128)}, u32[]{:S(2)}) copy-start(s32[61]{0:T(128)} %param.7) | copy-start | bytes 736
  114.3 0.9 copy-start.2
  128.4 1.8 %collective-permute-start.1 = (f32[72,896]{1,0:T(8,128)}, f32[72,896]{1,0:T(8,128)S(1)}, u32[]{:S(2)}, u32[]{:S(2)}) collective-permute-start(f32[72,896]{1,0:T(8,128)} %get-tuple-element.9), channel_id=1, source_target_pairs={{0,1},{1,0},{2,3},{3,2},{4,5},{5,4},{6,7},{7,6},{8,9},{9,8},{10,11... | collective-permute-start | bytes 774152 | tf_op jit(solution)/shard_map/ppermute | solution.py:263
  130.2 0.7 copy-start.3
